TPU v7x, 32 devices: a whole 2x2x4 slice. The times are simulated.
32 devices in a mesh: dp: 2 (over x), expert: 16 (over z, y, core).
Axes of the slice: x: 2, y: 2, z: 4, core: 2. Of those that a mesh axis runs over, the one named last changes fastest.
Arguments:
- tokens: bfloat16 [4096, 2048], P(('dp', 'expert')), may hold values from -160 to 160
- router_weight: bfloat16 [2048, 16], replicated, may hold values from -0.25 to 0.25
- route_ids: int32 [4096, 2], P(('dp', 'expert')), may hold values from 0 to 15, as said below
- gate_weight: bfloat16 [16, 768, 2048], P('expert', 'dp'), may hold values from -0.125 to 0.125
- up_weight: bfloat16 [16, 768, 2048], P('expert', 'dp'), may hold values from -0.125 to 0.125
- down_weight: bfloat16 [16, 768, 2048], P('expert', 'dp'), may hold values from -0.21875 to 0.21875
Outputs:
- mixture: bfloat16 [4096, 2048], P(('dp', 'expert'))
- z_loss: float32 [], replicated
Inputs may be any that keep to these rules, and one draw needn't show every extreme that they name: `route_ids`: each row names 2 different experts; among the rows of one device no expert is named more than 20 times, and one expert is named exactly 20 times by the rows of every device.
All inputs are finite; a program needn't handle non-finite values.
Results may differ from a plain program's by a relative error of at most 0.0057.
Values may be sent and summed in bfloat16 or wider, within the bound.
A program may use at most 64 MiB of HBM per device.

v0:
```python
import functools

import jax
import jax.numpy as jnp
from jax import lax
from jax.experimental import pallas as pl
from jax.experimental.pallas import tpu as pltpu
from jax.sharding import PartitionSpec as P

MESH = pl.DeviceIdType.MESH
F32 = jnp.float32
BF16 = jnp.bfloat16
TILE = 16
PLAN = (
    ("send", 0),
    ("send", 1),
    ("send", 2),
    ("send", 3),
    ("got", 0),
    ("load", 0),
    ("route", 0),
    ("own", 0),
    ("got", 1),
    ("own", 1),
    ("got", 2),
    ("peer", 2),
    ("own", 2),
    ("got", 3),
    ("peer", 1),
    ("end", 2),
    ("peer", 3),
    ("own", 3),
    ("end", 1),
    ("peer", 0),
    ("end", 3),
    ("loss", 0),
    ("end", 0),
    ("done", 2),
    ("done", 1),
    ("done", 3),
    ("done", 0),
)
PLAN_ONE = tuple((op, 0) for op in ('send', 'got', 'load', 'route', 'own', 'peer', 'end', 'loss', 'done'))


def dot(a, b, dims=((1,), (0,))):
    return lax.dot_general(a, b, (dims, ((), ())), preferred_element_type=F32)


def iota(shape, axis):
    return lax.broadcasted_iota(jnp.int32, shape, axis)


def kernel(
    n, dpn, cap, groups,
    tok_ref, router_ref, ids_ref, gate_hbm, up_hbm, down_hbm,
    mix_ref, z_ref,
    snd, rx, px, fin, ret, own, gate_ref, up_ref, down_ref, zsnd, zrx, zmid, zdp,
    d_send, d_recv, f_send, f_recv, p_send, p_recv, r_send, r_recv,
    z_send, z_recv, y_send, y_recv, w_sem,
    hi_ref, lo_ref, acc_ref,
):
    rows, width = tok_ref.shape
    topk = ids_ref.shape[0]
    size = n // groups
    mains = cap // TILE
    rest = cap - mains * TILE
    slot = 1
    while slot < rest:
        slot *= 2
    cuts = TILE // slot
    part = width // cuts
    base = mains * width
    me = lax.axis_index("expert")
    dp = lax.axis_index("dp")
    zone = me // size
    lane = me % size

    plan = PLAN if groups == 4 else PLAN_ONE
    SEND = [k for op, k in plan if op == 'send']
    tail = [k for op, k in plan if op == 'done']

    def zone_of(k):
        if groups == 4:
            return ((zone // 2 + k // 2) % 2) * 2 + (zone % 2 + k % 2) % 2
        return (zone + k) % groups

    def peer_of(j):
        return (dp + j) % dpn

    loads = [
        pltpu.make_async_copy(src.at[0], dst, w_sem.at[i])
        for i, (src, dst) in enumerate(
            ((gate_hbm, gate_ref), (up_hbm, up_ref), (down_hbm, down_ref))
        )
    ]
    for load in loads:
        load.start()

    barrier = pltpu.get_barrier_semaphore()

    def greet(j, c):
        pl.semaphore_signal(
            barrier, inc=1, device_id={"expert": (me + j) % n}, device_id_type=MESH
        )
        return c

    lax.fori_loop(1, n, greet, 0)
    for j in range(1, dpn):
        pl.semaphore_signal(
            barrier, inc=1, device_id={"dp": peer_of(j)}, device_id_type=MESH
        )

    hot_t = [(ids_ref[k : k + 1, :] == iota((n, rows), 0)) for k in range(topk)]
    all_t = sum(h.astype(F32) for h in hot_t).astype(BF16)
    upper = (iota((rows, rows), 0) < iota((rows, rows), 1)).astype(F32).astype(BF16)
    before_t = dot(all_t, upper)
    pos_t = [
        jnp.sum(jnp.where(h, before_t, 0.0), axis=0, keepdims=True).astype(jnp.int32)
        for h in hot_t
    ]

    def targets(ids, pos):
        out = []
        for m in range(mains):
            inside = (pos >= m * TILE) & (pos < (m + 1) * TILE)
            out.append(jnp.where(inside, ids * TILE + pos - m * TILE, -1))
        for c in range(cuts if rest else 0):
            inside = pos >= mains * TILE
            out.append(jnp.where(inside, ids * TILE + c * slot + pos - mains * TILE, -1))
        return out

    goal_t = [targets(ids_ref[k : k + 1, :], pos_t[k]) for k in range(topk)]
    row_at = iota((size * TILE, rows), 0)

    def dispatch(to, at):
        return pltpu.make_async_remote_copy(
            src_ref=snd.at[to], dst_ref=rx.at[dp, at],
            send_sem=d_send.at[to], recv_sem=d_recv.at[at],
            device_id={"expert": to}, device_id_type=MESH,
        )

    def forward(j, at, whose):
        return pltpu.make_async_remote_copy(
            src_ref=rx.at[dp, at], dst_ref=rx.at[whose, at],
            send_sem=f_send.at[peer_of(j), at], recv_sem=f_recv.at[whose, at],
            device_id={"dp": peer_of(j)}, device_id_type=MESH,
        )

    def send_group(k):
        first = zone_of(k) * size
        mine = pl.ds(first, size)

        def pick(i):
            at = row_at + first * TILE
            hit = at == goal_t[0][i]
            for c in range(1, topk):
                hit = hit | (at == goal_t[c][i])
            return hit.astype(F32).astype(BF16)

        for m in range(mains):
            snd[mine, :, m * width : (m + 1) * width] = (
                dot(pick(m), tok_ref[...]).astype(BF16).reshape(size, TILE, width)
            )
        if rest:
            extra = sum(
                dot(pick(mains + c), tok_ref[:, c * part : (c + 1) * part])
                for c in range(cuts)
            )
            snd[mine, :, base:] = extra.astype(BF16).reshape(size, TILE, part)
        if k == SEND[0]:
            pl.semaphore_wait(barrier, n - 1 + dpn - 1)

        def one(j, c):
            to = first + (lane + j) % size
            dispatch(to, me).start()
            return c

        lax.fori_loop(1 if k == 0 else 0, size, one, 0)
        if k == 0:
            rx[dp, me] = snd[me]
            for q in range(1, dpn):
                forward(q, me, dp).start()

    count = size * TILE
    at_row, at_col = iota((count, count), 0), iota((count, count), 1)
    per_cut = size * slot
    want = ((at_row % per_cut) // slot) * TILE + (at_row // per_cut) * slot + at_row % slot
    order = (at_col == want).astype(F32).astype(BF16)

    def natural(block):
        pieces = [
            block[:, :, m * width : (m + 1) * width].reshape(count, width)
            for m in range(mains)
        ]
        if rest:
            sorted_rows = dot(order, block[:, :, base:].reshape(count, part)).astype(BF16)
            pieces.append(
                jnp.concatenate(
                    [sorted_rows[c * per_cut : (c + 1) * per_cut] for c in range(cuts)],
                    axis=1,
                )
            )
        return pieces

    def blocks_of(rows_out, store):
        for m in range(mains):
            store(
                m * width, width,
                rows_out[m * count : (m + 1) * count].reshape(size, TILE, width),
            )
        if rest:
            tail = rows_out[mains * count :]
            stacked = jnp.concatenate(
                [tail[:, c * part : (c + 1) * part] for c in range(cuts)], axis=0
            )
            mixed = dot(order, stacked, ((0,), (0,))).astype(BF16)
            store(base, part, mixed.reshape(size, TILE, part))

    def expert(block):
        x = jnp.concatenate(natural(block), axis=0)
        gate = dot(x, gate_ref[...], ((1,), (1,)))
        up = dot(x, up_ref[...], ((1,), (1,)))
        hidden = (gate / (1.0 + jnp.exp(-gate)) * up).astype(BF16)
        return dot(hidden, down_ref[...])

    def partial_copy(j, t, whose):
        first = zone_of(t) * size
        return pltpu.make_async_remote_copy(
            src_ref=rx.at[peer_of(j), pl.ds(first, size)],
            dst_ref=px.at[whose, pl.ds(first, size)],
            send_sem=p_send.at[peer_of(j), t], recv_sem=p_recv.at[whose, t],
            device_id={"dp": peer_of(j)}, device_id_type=MESH,
        )

    def give_back(to, at):
        return pltpu.make_async_remote_copy(
            src_ref=fin.at[to], dst_ref=ret.at[at],
            send_sem=r_send.at[to], recv_sem=r_recv.at[at],
            device_id={"expert": to}, device_id_type=MESH,
        )

    def loss_copy(to, at):
        return pltpu.make_async_remote_copy(
            src_ref=zsnd, dst_ref=zrx.at[at],
            send_sem=z_send.at[to], recv_sem=z_recv.at[at],
            device_id={"expert": to}, device_id_type=MESH,
        )

    def loss_dp(j, whose):
        return pltpu.make_async_remote_copy(
            src_ref=zmid, dst_ref=zdp.at[whose],
            send_sem=y_send.at[peer_of(j)], recv_sem=y_recv.at[whose],
            device_id={"dp": peer_of(j)}, device_id_type=MESH,
        )

    def route():
        logits = dot(tok_ref[...], router_ref[...], ((1,), (1,)))
        top = jnp.max(logits, axis=1, keepdims=True)
        log_total = top + jnp.log(jnp.sum(jnp.exp(logits - top), axis=1, keepdims=True))
        local = jnp.sum(log_total * log_total, axis=0, keepdims=True)
        zsnd[...] = jnp.broadcast_to(local, zsnd.shape)
        zrx[me] = jnp.broadcast_to(local, zsnd.shape)

        def send_loss(j, c):
            loss_copy((me + j) % n, me).start()
            return c

        lax.fori_loop(1, n, send_loss, 0)

        same = (iota((n, n), 0) == iota((n, n), 1)).astype(F32).astype(BF16)
        hot = [dot(h.astype(F32).astype(BF16), same, ((0,), (0,))) > 0.5 for h in hot_t]
        ids = [
            jnp.sum(jnp.where(h, iota((rows, n), 1), 0), axis=1, keepdims=True) for h in hot
        ]
        chosen = [jnp.sum(jnp.where(h, logits, 0.0), axis=1, keepdims=True) for h in hot]
        high = functools.reduce(jnp.maximum, chosen)
        exps = [jnp.exp(c - high) for c in chosen]
        share = [e / sum(exps) for e in exps]
        all_hot = sum(h.astype(F32) for h in hot).astype(BF16)
        lower = (iota((rows, rows), 1) < iota((rows, rows), 0)).astype(F32).astype(BF16)
        before = dot(lower, all_hot)
        pos = [
            jnp.sum(jnp.where(h, before, 0.0), axis=1, keepdims=True).astype(jnp.int32)
            for h in hot
        ]
        goal = [targets(ids[k], pos[k]) for k in range(topk)]

        col_at = iota((rows, n * TILE), 1)
        for i in range(mains + (cuts if rest else 0)):
            w = sum(jnp.where(col_at == goal[k][i], share[k], 0.0) for k in range(topk))
            hi = w.astype(BF16)
            hi_ref[i] = hi
            lo_ref[i] = (w - hi.astype(F32)).astype(BF16)

    def arrive(k):
        first = zone_of(k) * size

        def one(j, c):
            at = first + (lane + j) % size
            dispatch(at, at).wait_recv()
            for q in range(1, dpn):
                forward(q, at, dp).start()
            return c

        lax.fori_loop(1 if k == 0 else 0, size, one, 0)

    def own_part(k):
        own[k] = expert(rx[dp, pl.ds(zone_of(k) * size, size)])

    def peer_part(k):
        first = zone_of(k) * size

        def one(q, c):
            whose = peer_of(q)

            def landed(j, c2):
                forward(q, first + (lane + j) % size, whose).wait_recv()
                return c2

            lax.fori_loop(0, size, landed, 0)
            out = expert(rx[whose, pl.ds(first, size)]).astype(BF16)

            def store(start, wide, value):
                rx[whose, pl.ds(first, size), :, start : start + wide] = value

            blocks_of(out, store)
            partial_copy(q, k, dp).start()
            return c

        lax.fori_loop(1, dpn, one, 0)

    def finish(k):
        first = zone_of(k) * size
        total = own[k]
        for q in range(1, dpn):
            partial_copy(q, k, peer_of(q)).wait_recv()
            block = px[peer_of(q), pl.ds(first, size)]
            total = total + jnp.concatenate(natural(block), axis=0).astype(F32)

        def store(start, wide, value):
            fin[pl.ds(first, size), :, start : start + wide] = value

        blocks_of(total.astype(BF16), store)

        def back(j, c):
            give_back(first + (lane + j) % size, me).start()
            return c

        lax.fori_loop(1 if k == 0 else 0, size, back, 0)
        if k == 0:
            ret[me] = fin[me]

    def take(k):
        first = zone_of(k) * size
        mine = pl.ds(first, size)

        def one(j, c):
            at = first + (lane + j) % size
            give_back(at, at).wait_recv()
            return c

        lax.fori_loop(1 if k == 0 else 0, size, one, 0)
        start = zone_of(k) * size * TILE
        sub = (iota((n * TILE, size * TILE), 0) == iota((n * TILE, size * TILE), 1) + start)
        sub = sub.astype(F32).astype(BF16)

        def cut(i):
            hi = dot(hi_ref[i], sub).astype(BF16)
            lo = dot(lo_ref[i], sub).astype(BF16)
            return jnp.concatenate([hi, lo], axis=1)

        def twice(x):
            return jnp.concatenate([x, x], axis=0)

        main_w = [cut(m) for m in range(mains)]
        for c in range(cuts):
            cols = slice(c * part, (c + 1) * part)
            acc = 0.0 if k == tail[0] else acc_ref[:, cols]
            for m in range(mains):
                seen = ret[mine, :, m * width + c * part : m * width + (c + 1) * part]
                acc = acc + dot(main_w[m], twice(seen.reshape(count, part)))
            if rest:
                seen = ret[mine, :, base:].reshape(count, part)
                acc = acc + dot(cut(mains + c), twice(seen))
            if k == tail[-1]:
                mix_ref[:, cols] = acc.astype(BF16)
            else:
                acc_ref[:, cols] = acc

    def loads_in(k):
        for load in loads:
            load.wait()

    def gather_loss():
        def loss_in(j, c):
            at = (me + j) % n
            loss_copy(at, at).wait_recv()
            return c

        lax.fori_loop(1, n, loss_in, 0)
        mid = zrx[0]
        for i in range(1, n):
            mid = mid + zrx[i]
        zmid[...] = mid
        zdp[dp] = mid

        for q in range(1, dpn):
            loss_dp(q, dp).start()

    steps = {
        "send": send_group, "got": arrive, "own": own_part, "peer": peer_part,
        "end": finish, "done": take, "load": loads_in,
        "route": lambda k: route(), "loss": lambda k: gather_loss(),
    }
    for op, k in plan:
        steps[op](k)

    loss = zdp[dp]
    for q in range(1, dpn):
        loss_dp(q, peer_of(q)).wait_recv()
        loss = loss + zdp[peer_of(q)]
    z_ref[...] = loss[0:1, 0:1] / F32(rows * n * dpn)

    def sent(j, c):
        to = (me + j) % n
        dispatch(to, me).wait_send()
        loss_copy(to, me).wait_send()
        give_back(to, me).wait_send()
        return c

    lax.fori_loop(1, n, sent, 0)
    for q in range(1, dpn):
        loss_dp(q, dp).wait_send()

        def forwarded(at, c, q=q):
            forward(q, at, dp).wait_send()
            return c

        lax.fori_loop(0, n, forwarded, 0)

        def parted(t, c, q=q):
            partial_copy(q, t, dp).wait_send()
            return c

        lax.fori_loop(0, groups, parted, 0)


def on_device(n, dpn, tokens, router_weight, route_ids, gate_weight, up_weight, down_weight):
    rows, width = tokens.shape
    topk = route_ids.shape[1]
    experts = router_weight.shape[1]
    assert experts == n and gate_weight.shape[0] == 1
    cap = 5 * rows * topk // (4 * experts)
    groups = 4 if n % 4 == 0 else 1
    mains, rest = cap // TILE, cap % TILE
    slot = 1
    while slot < rest:
        slot *= 2
    block = mains * width + (width * slot // TILE if rest else 0)
    size = n // groups
    in_rows = size * TILE * mains + (size * slot if rest else 0)
    hidden = gate_weight.shape[1]
    vmem = pl.BlockSpec(memory_space=pltpu.VMEM)
    hbm = pl.BlockSpec(memory_space=pl.ANY)
    dma = pltpu.SemaphoreType.DMA
    mixture, loss = pl.pallas_call(
        functools.partial(kernel, n, dpn, cap, groups),
        out_shape=(
            pltpu.VMEM((rows, width), BF16),
            jax.ShapeDtypeStruct((1, 1), F32),
        ),
        in_specs=[vmem, vmem, vmem, hbm, hbm, hbm],
        out_specs=(vmem, vmem),
        scratch_shapes=[
            pltpu.VMEM((n, TILE, block), BF16),
            pltpu.VMEM((dpn, n, TILE, block), BF16),
            pltpu.VMEM((dpn, n, TILE, block), BF16),
            pltpu.VMEM((n, TILE, block), BF16),
            pltpu.VMEM((n, TILE, block), BF16),
            pltpu.VMEM((groups, in_rows, width), F32),
            pltpu.VMEM((hidden, width), BF16),
            pltpu.VMEM((hidden, width), BF16),
            pltpu.VMEM((hidden, width), BF16),
            pltpu.VMEM((8, 128), F32),
            pltpu.VMEM((n, 8, 128), F32),
            pltpu.VMEM((8, 128), F32),
            pltpu.VMEM((dpn, 8, 128), F32),
            dma((n,)), dma((n,)), dma((dpn, n)), dma((dpn, n)),
            dma((dpn, groups)), dma((dpn, groups)), dma((n,)), dma((n,)),
            dma((n,)), dma((n,)), dma((dpn,)), dma((dpn,)), dma((3,)),
            pltpu.VMEM((mains + (TILE // slot if rest else 0), rows, n * TILE), BF16),
            pltpu.VMEM((mains + (TILE // slot if rest else 0), rows, n * TILE), BF16),
            pltpu.VMEM((rows, width), F32),
        ],
        compiler_params=pltpu.CompilerParams(
            collective_id=0, has_side_effects=True, vmem_limit_bytes=60 * 1024 * 1024
        ),
    )(tokens, router_weight.T, route_ids.T, gate_weight, up_weight, down_weight)
    return mixture, loss[0, 0]


def solution(mesh):
    in_specs = (
        P(("dp", "expert"), None),
        P(),
        P(("dp", "expert"), None),
        P("expert", "dp", None),
        P("expert", "dp", None),
        P("expert", "dp", None),
    )
    out_specs = (P(("dp", "expert"), None), P())
    return jax.shard_map(
        functools.partial(on_device, mesh.shape["expert"], mesh.shape["dp"]),
        mesh=mesh, in_specs=in_specs, out_specs=out_specs, check_vma=False,
    )
```

profile of v0, /device:TPU:0, one launch (start us, length us, event | category | flops | bytes accessed | tf_op | source)
XLA Modules:
  0.0 86.4 jit_solution(14905980938697300551)
XLA Ops:
  0.6 83.3 %shard_map.77 = (bf16[128,2048]{1,0:T(8,128)(2,1)S(1)}, f32[1,1]{1,0:T(1,128)}) custom-call(bf16[128,2048]{1,0:T(8,128)(2,1)} %tok_ref.1, bf16[16,2048]{1,0:T(8,128)(2,1)} %bitcast.3, s32[2,128]{1,0:T(2,128)} %bitcast.4, bf16[1,384,2048]{2,1,0:T(8,128)(2,1)} %gate_hbm.1, bf16[1,384,2048]{2,1,0:T(8,128)(2,1)} %up_hbm.1, bf16[1,384,2048]{2,1,0:T(8,128)(2,1)} %down_hbm.1), custom_call_target="tpu_custom_call" | custom-call | tf_op jit(solution)/shard_map/pallas_call | solution.py:467
  83.9 0.8 copy.10
where the time goes:
time: 87.3 us; the launch traced here: 86.4 us
  Pallas kernels  83.3 us (95%)
  between operations  2.33 us (3%)
    pallas_call x1, Pallas kernels, on_device(): pl.pallas_call(functools.partial(kernel, n, dpn, cap, groups), out_shape=...  83.3 us

commit v1 on v0

--- a/solution.py
+++ b/solution.py
@@ -11,36 +11,25 @@
 F32 = jnp.float32
 BF16 = jnp.bfloat16
 TILE = 16
+NO = None
 PLAN = (
-    ("send", 0),
-    ("send", 1),
-    ("send", 2),
-    ("send", 3),
-    ("got", 0),
-    ("load", 0),
-    ("route", 0),
-    ("own", 0),
-    ("got", 1),
-    ("own", 1),
-    ("got", 2),
-    ("peer", 2),
-    ("own", 2),
-    ("got", 3),
-    ("peer", 1),
-    ("end", 2),
-    ("peer", 3),
-    ("own", 3),
-    ("end", 1),
-    ("peer", 0),
-    ("end", 3),
-    ("loss", 0),
-    ("end", 0),
-    ("done", 2),
-    ("done", 1),
-    ("done", 3),
-    ("done", 0),
+    ("send", 0), ("send", 2), ("send", 1), ("send", 3),
+    ("load", 0), ("got", 0), ("own", 0),
+    ("got", (1, 2), 0), ("got", (1, 2), 1), ("route", 0), ("got", (1, 2), 2), ("got", (1, 2), 3),
+    ("own", (1, 2)), ("peer", 0),
+    ("got", (2, 1), 0), ("got", (2, 1), 1), ("got", (2, 1), 2), ("got", (2, 1), 3),
+    ("own", (2, 1)), ("weigh", 0), ("peer", (1, 2)), ("part", (NO, 2)),
+    ("got", (3, NO), 0), ("got", (3, NO), 1), ("got", (3, NO), 2), ("got", (3, NO), 3),
+    ("peer", (2, 1)), ("part", (2, NO)),
+    ("got", (NO, 3), 0), ("got", (NO, 3), 1), ("end", (NO, 2)), ("got", (NO, 3), 2), ("got", (NO, 3), 3),
+    ("part", (NO, 1)), ("own", 3), ("peer", 3), ("part", 3), ("part", (1, NO)), ("part", 0),
+    ("end", (2, NO)), ("end", (3, 1)), ("loss", 0), ("done", (2,)), ("end", (1, 3)), ("end", 0),
+    ("drain", 0), ("done", (1, 3)), ("done", (0,)),
 )
-PLAN_ONE = tuple((op, 0) for op in ('send', 'got', 'load', 'route', 'own', 'peer', 'end', 'loss', 'done'))
+PLAN_ONE = tuple(
+    (op, (0,) if op == "done" else 0)
+    for op in ("send", "load", "got", "route", "weigh", "own", "peer", "part", "end", "loss", "drain", "done")
+)
 
 
 def dot(a, b, dims=((1,), (0,))):
@@ -58,7 +47,7 @@
     snd, rx, px, fin, ret, own, gate_ref, up_ref, down_ref, zsnd, zrx, zmid, zdp,
     d_send, d_recv, f_send, f_recv, p_send, p_recv, r_send, r_recv,
     z_send, z_recv, y_send, y_recv, w_sem,
-    hi_ref, lo_ref, acc_ref,
+    hi_ref, lo_ref, w_ref, acc_ref,
 ):
     rows, width = tok_ref.shape
     topk = ids_ref.shape[0]
@@ -77,8 +66,12 @@
     lane = me % size
 
     plan = PLAN if groups == 4 else PLAN_ONE
-    SEND = [k for op, k in plan if op == 'send']
-    tail = [k for op, k in plan if op == 'done']
+    inner = ((zone + 1) // 2) % 2 if groups == 4 else 0
+    first_send = [step[1] for step in plan if step[0] == "send"][0]
+    tail = [step[1] for step in plan if step[0] == "done"]
+
+    def home(k):
+        return isinstance(k, int) and k == 0
 
     def zone_of(k):
         if groups == 4:
@@ -111,6 +104,8 @@
             barrier, inc=1, device_id={"dp": peer_of(j)}, device_id_type=MESH
         )
 
+    with jax.named_scope("begin"):
+        pass
     hot_t = [(ids_ref[k : k + 1, :] == iota((n, rows), 0)) for k in range(topk)]
     all_t = sum(h.astype(F32) for h in hot_t).astype(BF16)
     upper = (iota((rows, rows), 0) < iota((rows, rows), 1)).astype(F32).astype(BF16)
@@ -168,7 +163,7 @@
                 for c in range(cuts)
             )
             snd[mine, :, base:] = extra.astype(BF16).reshape(size, TILE, part)
-        if k == SEND[0]:
+        if k == first_send:
             pl.semaphore_wait(barrier, n - 1 + dpn - 1)
 
         def one(j, c):
@@ -176,7 +171,7 @@
             dispatch(to, me).start()
             return c
 
-        lax.fori_loop(1 if k == 0 else 0, size, one, 0)
+        lax.fori_loop(1 if home(k) else 0, size, one, 0)
         if k == 0:
             rx[dp, me] = snd[me]
             for q in range(1, dpn):
@@ -293,17 +288,21 @@
             hi_ref[i] = hi
             lo_ref[i] = (w - hi.astype(F32)).astype(BF16)
 
-    def arrive(k):
+    def arrive(k, part=None):
         first = zone_of(k) * size
 
         def one(j, c):
-            at = first + (lane + j) % size
+            at = first + (lane + size - j) % size
             dispatch(at, at).wait_recv()
             for q in range(1, dpn):
                 forward(q, at, dp).start()
             return c
 
-        lax.fori_loop(1 if k == 0 else 0, size, one, 0)
+        if part is None:
+            lax.fori_loop(1 if home(k) else 0, size, one, 0)
+        else:
+            quarter = size // 4
+            lax.fori_loop(part * quarter, (part + 1) * quarter, one, 0)
 
     def own_part(k):
         own[k] = expert(rx[dp, pl.ds(zone_of(k) * size, size)])
@@ -325,10 +324,13 @@
                 rx[whose, pl.ds(first, size), :, start : start + wide] = value
 
             blocks_of(out, store)
+            return c
+
+        lax.fori_loop(1, dpn, one, 0)
+
+    def send_part(k):
+        for q in range(1, dpn):
             partial_copy(q, k, dp).start()
-            return c
-
-        lax.fori_loop(1, dpn, one, 0)
 
     def finish(k):
         first = zone_of(k) * size
@@ -347,43 +349,49 @@
             give_back(first + (lane + j) % size, me).start()
             return c
 
-        lax.fori_loop(1 if k == 0 else 0, size, back, 0)
-        if k == 0:
+        lax.fori_loop(1 if home(k) else 0, size, back, 0)
+        if home(k):
             ret[me] = fin[me]
 
-    def take(k):
-        first = zone_of(k) * size
-        mine = pl.ds(first, size)
-
-        def one(j, c):
-            at = first + (lane + j) % size
-            give_back(at, at).wait_recv()
-            return c
-
-        lax.fori_loop(1 if k == 0 else 0, size, one, 0)
+    def cut(i, k):
         start = zone_of(k) * size * TILE
         sub = (iota((n * TILE, size * TILE), 0) == iota((n * TILE, size * TILE), 1) + start)
         sub = sub.astype(F32).astype(BF16)
-
-        def cut(i):
-            hi = dot(hi_ref[i], sub).astype(BF16)
-            lo = dot(lo_ref[i], sub).astype(BF16)
-            return jnp.concatenate([hi, lo], axis=1)
+        hi = dot(hi_ref[i], sub).astype(BF16)
+        lo = dot(lo_ref[i], sub).astype(BF16)
+        return jnp.concatenate([hi, lo], axis=1)
+
+    def weigh(k):
+        for i in range(mains + (cuts if rest else 0)):
+            for k in range(groups):
+                w_ref[i, k] = cut(i, k)
+
+    def take(ks):
+        for k in ks:
+            first = zone_of(k) * size
+
+            def one(j, c, first=first):
+                at = first + (lane + size - j) % size
+                give_back(at, at).wait_recv()
+                return c
+
+            lax.fori_loop(1 if home(k) else 0, size, one, 0)
 
         def twice(x):
             return jnp.concatenate([x, x], axis=0)
 
-        main_w = [cut(m) for m in range(mains)]
         for c in range(cuts):
             cols = slice(c * part, (c + 1) * part)
-            acc = 0.0 if k == tail[0] else acc_ref[:, cols]
-            for m in range(mains):
-                seen = ret[mine, :, m * width + c * part : m * width + (c + 1) * part]
-                acc = acc + dot(main_w[m], twice(seen.reshape(count, part)))
-            if rest:
-                seen = ret[mine, :, base:].reshape(count, part)
-                acc = acc + dot(cut(mains + c), twice(seen))
-            if k == tail[-1]:
+            acc = 0.0 if ks == tail[0] else acc_ref[:, cols]
+            for k in ks:
+                mine = pl.ds(zone_of(k) * size, size)
+                for m in range(mains):
+                    seen = ret[mine, :, m * width + c * part : m * width + (c + 1) * part]
+                    acc = acc + dot(w_ref[m, k], twice(seen.reshape(count, part)))
+                if rest:
+                    seen = ret[mine, :, base:].reshape(count, part)
+                    acc = acc + dot(w_ref[mains + c, k], twice(seen))
+            if ks == tail[-1]:
                 mix_ref[:, cols] = acc.astype(BF16)
             else:
                 acc_ref[:, cols] = acc
@@ -408,42 +416,55 @@
         for q in range(1, dpn):
             loss_dp(q, dp).start()
 
+    def drain(k):
+        def sent(j, c):
+            to = (me + j) % n
+            dispatch(to, me).wait_send()
+            loss_copy(to, me).wait_send()
+            return c
+
+        lax.fori_loop(1, n, sent, 0)
+        for q in range(1, dpn):
+            loss_dp(q, dp).wait_send()
+
+            def forwarded(at, c, q=q):
+                forward(q, at, dp).wait_send()
+                return c
+
+            lax.fori_loop(0, n, forwarded, 0)
+
+            def parted(t, c, q=q):
+                partial_copy(q, t, dp).wait_send()
+                return c
+
+            lax.fori_loop(0, groups, parted, 0)
+        loss = zdp[dp]
+        for q in range(1, dpn):
+            loss_dp(q, peer_of(q)).wait_recv()
+            loss = loss + zdp[peer_of(q)]
+        z_ref[...] = loss[0:1, 0:1] / F32(rows * n * dpn)
+
     steps = {
         "send": send_group, "got": arrive, "own": own_part, "peer": peer_part,
-        "end": finish, "done": take, "load": loads_in,
-        "route": lambda k: route(), "loss": lambda k: gather_loss(),
+        "part": send_part, "end": finish, "done": take, "load": loads_in,
+        "route": lambda k: route(), "loss": lambda k: gather_loss(), "weigh": weigh, "drain": drain,
     }
-    for op, k in plan:
-        steps[op](k)
-
-    loss = zdp[dp]
-    for q in range(1, dpn):
-        loss_dp(q, peer_of(q)).wait_recv()
-        loss = loss + zdp[peer_of(q)]
-    z_ref[...] = loss[0:1, 0:1] / F32(rows * n * dpn)
-
-    def sent(j, c):
-        to = (me + j) % n
-        dispatch(to, me).wait_send()
-        loss_copy(to, me).wait_send()
-        give_back(to, me).wait_send()
+    for op, at, *more in plan:
+        with jax.named_scope(f"{op}_{at}_{more}"):
+            if op == "done" or not isinstance(at, tuple):
+                steps[op](at, *more)
+            elif None in at:
+                chosen = at[0] if at[1] is None else at[1]
+                pl.when(inner == at.index(chosen))(functools.partial(steps[op], chosen, *more))
+            else:
+                steps[op](at[0] + inner * (at[1] - at[0]), *more)
+
+    def returned(j, c):
+        give_back((me + j) % n, me).wait_send()
         return c
 
-    lax.fori_loop(1, n, sent, 0)
-    for q in range(1, dpn):
-        loss_dp(q, dp).wait_send()
-
-        def forwarded(at, c, q=q):
-            forward(q, at, dp).wait_send()
-            return c
-
-        lax.fori_loop(0, n, forwarded, 0)
-
-        def parted(t, c, q=q):
-            partial_copy(q, t, dp).wait_send()
-            return c
-
-        lax.fori_loop(0, groups, parted, 0)
+    with jax.named_scope("finalwait"):
+        lax.fori_loop(1, n, returned, 0)
 
 
 def on_device(n, dpn, tokens, router_weight, route_ids, gate_weight, up_weight, down_weight):
@@ -491,6 +512,7 @@
             dma((n,)), dma((n,)), dma((dpn,)), dma((dpn,)), dma((3,)),
             pltpu.VMEM((mains + (TILE // slot if rest else 0), rows, n * TILE), BF16),
             pltpu.VMEM((mains + (TILE // slot if rest else 0), rows, n * TILE), BF16),
+            pltpu.VMEM((mains + (TILE // slot if rest else 0), groups, rows, 2 * size * TILE), BF16),
             pltpu.VMEM((rows, width), F32),
         ],
         compiler_params=pltpu.CompilerParams(

time: 87.3 us -> 81.5 us (0.934)
  the two profiles are of different devices: /device:TPU:0 before, /device:TPU:9 now
where the time goes in v1:
time: 81.5 us; the launch traced here: 81.3 us
  Pallas kernels  78.2 us (96%)
  between operations  2.33 us (3%)
    pallas_call x1, Pallas kernels, on_device(): pl.pallas_call(functools.partial(kernel, n, dpn, cap, groups), out_shape=...  78.2 us

profile of v1, /device:TPU:9, one launch (start us, length us, event | category | flops | bytes accessed | tf_op | source)
XLA Modules:
  0.0 81.3 jit_solution(14967468539112932085)
XLA Ops:
  0.6 78.2 %shard_map.77 = (bf16[128,2048]{1,0:T(8,128)(2,1)S(1)}, f32[1,1]{1,0:T(1,128)}) custom-call(bf16[128,2048]{1,0:T(8,128)(2,1)} %tok_ref.1, bf16[16,2048]{1,0:T(8,128)(2,1)} %bitcast.3, s32[2,128]{1,0:T(2,128)} %bitcast.4, bf16[1,384,2048]{2,1,0:T(8,128)(2,1)} %gate_hbm.1, bf16[1,384,2048]{2,1,0:T(8,128)(2,1)} %up_hbm.1, bf16[1,384,2048]{2,1,0:T(8,128)(2,1)} %down_hbm.1), custom_call_target="tpu_custom_call" | custom-call | tf_op jit(solution)/shard_map/pallas_call | solution.py:488
  78.9 0.8 copy.10

commit v2 on v1

--- a/solution.py
+++ b/solution.py
@@ -13,21 +13,22 @@
 TILE = 16
 NO = None
 PLAN = (
-    ("send", 0), ("send", 2), ("send", 1), ("send", 3),
+    ("send", (2, 1), True), ("send", 0), ("send", (1, 2)), ("send", 3),
     ("load", 0), ("got", 0), ("own", 0),
     ("got", (1, 2), 0), ("got", (1, 2), 1), ("route", 0), ("got", (1, 2), 2), ("got", (1, 2), 3),
     ("own", (1, 2)), ("peer", 0),
-    ("got", (2, 1), 0), ("got", (2, 1), 1), ("got", (2, 1), 2), ("got", (2, 1), 3),
-    ("own", (2, 1)), ("weigh", 0), ("peer", (1, 2)), ("part", (NO, 2)),
-    ("got", (3, NO), 0), ("got", (3, NO), 1), ("got", (3, NO), 2), ("got", (3, NO), 3),
-    ("peer", (2, 1)), ("part", (2, NO)),
-    ("got", (NO, 3), 0), ("got", (NO, 3), 1), ("end", (NO, 2)), ("got", (NO, 3), 2), ("got", (NO, 3), 3),
-    ("part", (NO, 1)), ("own", 3), ("peer", 3), ("part", 3), ("part", (1, NO)), ("part", 0),
-    ("end", (2, NO)), ("end", (3, 1)), ("loss", 0), ("done", (2,)), ("end", (1, 3)), ("end", 0),
-    ("drain", 0), ("done", (1, 3)), ("done", (0,)),
+    ("got", (2, 1), 0), ("got", (2, 1), 1),
+    ("weigh", 0), ("peer", (1, 2)), ("part", (NO, 2)),
+    ("got", (2, NO), 2), ("got", (2, NO), 3), ("own", (2, NO)),
+    ("got", 3, 0), ("got", 3, 1), ("got", 3, 2), ("got", 3, 3),
+    ("peer", (2, NO)), ("part", (2, NO)), ("got", (NO, 1), 2), ("got", (NO, 1), 3),
+    ("own", 3), ("end", (NO, 2)), ("own", (NO, 1)), ("peer", 3), ("part", 3), ("part", (1, NO)),
+    ("peer", (NO, 1)), ("part", (NO, 1)), ("part", 0), ("end", (2, NO)),
+    ("end", 3), ("loss", 0), ("done", (2,)), ("end", 1), ("end", 0),
+    ("drain", 0), ("done", (3,)), ("done", (1,)), ("done", (0,)),
 )
 PLAN_ONE = tuple(
-    (op, (0,) if op == "done" else 0)
+    (op, (0,) if op == "done" else 0) + ((True,) if op == "send" else ())
     for op in ("send", "load", "got", "route", "weigh", "own", "peer", "part", "end", "loss", "drain", "done")
 )
 
@@ -42,15 +43,15 @@
 
 def kernel(
     n, dpn, cap, groups,
-    tok_ref, router_ref, ids_ref, gate_hbm, up_hbm, down_hbm,
+    tok_hbm, router_hbm, ids_hbm, gate_hbm, up_hbm, down_hbm,
     mix_ref, z_ref,
-    snd, rx, px, fin, ret, own, gate_ref, up_ref, down_ref, zsnd, zrx, zmid, zdp,
+    tok_ref, router_ref, ids_ref, snd, rx, px, fin, ret, own, ffn_ref, zsnd, zrx, zmid, zdp,
     d_send, d_recv, f_send, f_recv, p_send, p_recv, r_send, r_recv,
-    z_send, z_recv, y_send, y_recv, w_sem,
-    hi_ref, lo_ref, w_ref, acc_ref,
+    z_send, z_recv, y_send, y_recv, w_sem, i_sem,
+    hi_ref, lo_ref, w_ref, acc_ref, zout, o_sem,
 ):
-    rows, width = tok_ref.shape
-    topk = ids_ref.shape[0]
+    rows, width = tok_hbm.shape
+    topk = ids_hbm.shape[0]
     size = n // groups
     mains = cap // TILE
     rest = cap - mains * TILE
@@ -67,7 +68,6 @@
 
     plan = PLAN if groups == 4 else PLAN_ONE
     inner = ((zone + 1) // 2) % 2 if groups == 4 else 0
-    first_send = [step[1] for step in plan if step[0] == "send"][0]
     tail = [step[1] for step in plan if step[0] == "done"]
 
     def home(k):
@@ -81,15 +81,21 @@
     def peer_of(j):
         return (dp + j) % dpn
 
-    loads = [
-        pltpu.make_async_copy(src.at[0], dst, w_sem.at[i])
+    def landed(ref, sem):
+        pltpu.make_async_copy(ref, ref, sem).wait()
+
+    inputs = [
+        pltpu.make_async_copy(src, dst, i_sem.at[i])
         for i, (src, dst) in enumerate(
-            ((gate_hbm, gate_ref), (up_hbm, up_ref), (down_hbm, down_ref))
+            ((ids_hbm, ids_ref), (tok_hbm, tok_ref), (router_hbm, router_ref))
         )
     ]
-    for load in loads:
+    for load in inputs:
         load.start()
-
+    for i, src in enumerate((gate_hbm, up_hbm, down_hbm)):
+        pltpu.make_async_copy(src.at[0], ffn_ref.at[i], w_sem).start()
+
+    z_copy = pltpu.make_async_copy(zout, z_ref, o_sem)
     barrier = pltpu.get_barrier_semaphore()
 
     def greet(j, c):
@@ -104,8 +110,7 @@
             barrier, inc=1, device_id={"dp": peer_of(j)}, device_id_type=MESH
         )
 
-    with jax.named_scope("begin"):
-        pass
+    inputs[0].wait()
     hot_t = [(ids_ref[k : k + 1, :] == iota((n, rows), 0)) for k in range(topk)]
     all_t = sum(h.astype(F32) for h in hot_t).astype(BF16)
     upper = (iota((rows, rows), 0) < iota((rows, rows), 1)).astype(F32).astype(BF16)
@@ -125,24 +130,26 @@
             out.append(jnp.where(inside, ids * TILE + c * slot + pos - mains * TILE, -1))
         return out
 
+    inputs[1].wait()
+    inputs[2].wait()
     goal_t = [targets(ids_ref[k : k + 1, :], pos_t[k]) for k in range(topk)]
     row_at = iota((size * TILE, rows), 0)
 
     def dispatch(to, at):
         return pltpu.make_async_remote_copy(
             src_ref=snd.at[to], dst_ref=rx.at[dp, at],
-            send_sem=d_send.at[to], recv_sem=d_recv.at[at],
+            send_sem=d_send, recv_sem=d_recv.at[at],
             device_id={"expert": to}, device_id_type=MESH,
         )
 
     def forward(j, at, whose):
         return pltpu.make_async_remote_copy(
             src_ref=rx.at[dp, at], dst_ref=rx.at[whose, at],
-            send_sem=f_send.at[peer_of(j), at], recv_sem=f_recv.at[whose, at],
+            send_sem=f_send, recv_sem=f_recv.at[dpn - 1 - j, at // size],
             device_id={"dp": peer_of(j)}, device_id_type=MESH,
         )
 
-    def send_group(k):
+    def send_group(k, entry=False):
         first = zone_of(k) * size
         mine = pl.ds(first, size)
 
@@ -163,7 +170,7 @@
                 for c in range(cuts)
             )
             snd[mine, :, base:] = extra.astype(BF16).reshape(size, TILE, part)
-        if k == first_send:
+        if entry:
             pl.semaphore_wait(barrier, n - 1 + dpn - 1)
 
         def one(j, c):
@@ -172,7 +179,7 @@
             return c
 
         lax.fori_loop(1 if home(k) else 0, size, one, 0)
-        if k == 0:
+        if home(k):
             rx[dp, me] = snd[me]
             for q in range(1, dpn):
                 forward(q, me, dp).start()
@@ -214,38 +221,40 @@
 
     def expert(block):
         x = jnp.concatenate(natural(block), axis=0)
-        gate = dot(x, gate_ref[...], ((1,), (1,)))
-        up = dot(x, up_ref[...], ((1,), (1,)))
+        gate = dot(x, ffn_ref[0], ((1,), (1,)))
+        up = dot(x, ffn_ref[1], ((1,), (1,)))
         hidden = (gate / (1.0 + jnp.exp(-gate)) * up).astype(BF16)
-        return dot(hidden, down_ref[...])
-
-    def partial_copy(j, t, whose):
-        first = zone_of(t) * size
+        return dot(hidden, ffn_ref[2])
+
+    def partial_copy(j, t, half):
+        if half is None:
+            mine = pl.ds(zone_of(t) * size, size)
+        else:
+            mine = pl.ds(zone_of(t) * size + half * (size // 2), size // 2)
         return pltpu.make_async_remote_copy(
-            src_ref=rx.at[peer_of(j), pl.ds(first, size)],
-            dst_ref=px.at[whose, pl.ds(first, size)],
-            send_sem=p_send.at[peer_of(j), t], recv_sem=p_recv.at[whose, t],
+            src_ref=rx.at[peer_of(j), mine], dst_ref=px.at[dp, mine],
+            send_sem=p_send, recv_sem=p_recv.at[dpn - 1 - j, zone_of(t)],
             device_id={"dp": peer_of(j)}, device_id_type=MESH,
         )
 
     def give_back(to, at):
         return pltpu.make_async_remote_copy(
             src_ref=fin.at[to], dst_ref=ret.at[at],
-            send_sem=r_send.at[to], recv_sem=r_recv.at[at],
+            send_sem=r_send, recv_sem=r_recv.at[at // size],
             device_id={"expert": to}, device_id_type=MESH,
         )
 
     def loss_copy(to, at):
         return pltpu.make_async_remote_copy(
             src_ref=zsnd, dst_ref=zrx.at[at],
-            send_sem=z_send.at[to], recv_sem=z_recv.at[at],
+            send_sem=z_send, recv_sem=z_recv,
             device_id={"expert": to}, device_id_type=MESH,
         )
 
     def loss_dp(j, whose):
         return pltpu.make_async_remote_copy(
             src_ref=zmid, dst_ref=zdp.at[whose],
-            send_sem=y_send.at[peer_of(j)], recv_sem=y_recv.at[whose],
+            send_sem=y_send, recv_sem=y_recv,
             device_id={"dp": peer_of(j)}, device_id_type=MESH,
         )
 
@@ -313,11 +322,7 @@
         def one(q, c):
             whose = peer_of(q)
 
-            def landed(j, c2):
-                forward(q, first + (lane + j) % size, whose).wait_recv()
-                return c2
-
-            lax.fori_loop(0, size, landed, 0)
+            landed(rx.at[whose, pl.ds(first, size)], f_recv.at[q - 1, zone_of(k)])
             out = expert(rx[whose, pl.ds(first, size)]).astype(BF16)
 
             def store(start, wide, value):
@@ -328,15 +333,15 @@
 
         lax.fori_loop(1, dpn, one, 0)
 
-    def send_part(k):
+    def send_part(k, half=None):
         for q in range(1, dpn):
-            partial_copy(q, k, dp).start()
+            partial_copy(q, k, half).start()
 
     def finish(k):
         first = zone_of(k) * size
         total = own[k]
         for q in range(1, dpn):
-            partial_copy(q, k, peer_of(q)).wait_recv()
+            landed(px.at[peer_of(q), pl.ds(first, size)], p_recv.at[q - 1, zone_of(k)])
             block = px[peer_of(q), pl.ds(first, size)]
             total = total + jnp.concatenate(natural(block), axis=0).astype(F32)
 
@@ -368,14 +373,8 @@
 
     def take(ks):
         for k in ks:
-            first = zone_of(k) * size
-
-            def one(j, c, first=first):
-                at = first + (lane + size - j) % size
-                give_back(at, at).wait_recv()
-                return c
-
-            lax.fori_loop(1 if home(k) else 0, size, one, 0)
+            here = pl.ds(zone_of(k) * size, size - 1 if home(k) else size)
+            landed(ret.at[here], r_recv.at[zone_of(k)])
 
         def twice(x):
             return jnp.concatenate([x, x], axis=0)
@@ -397,16 +396,10 @@
                 acc_ref[:, cols] = acc
 
     def loads_in(k):
-        for load in loads:
-            load.wait()
+        landed(ffn_ref, w_sem)
 
     def gather_loss():
-        def loss_in(j, c):
-            at = (me + j) % n
-            loss_copy(at, at).wait_recv()
-            return c
-
-        lax.fori_loop(1, n, loss_in, 0)
+        landed(zrx.at[pl.ds(0, n - 1)], z_recv)
         mid = zrx[0]
         for i in range(1, n):
             mid = mid + zrx[i]
@@ -417,32 +410,17 @@
             loss_dp(q, dp).start()
 
     def drain(k):
-        def sent(j, c):
-            to = (me + j) % n
-            dispatch(to, me).wait_send()
-            loss_copy(to, me).wait_send()
-            return c
-
-        lax.fori_loop(1, n, sent, 0)
-        for q in range(1, dpn):
-            loss_dp(q, dp).wait_send()
-
-            def forwarded(at, c, q=q):
-                forward(q, at, dp).wait_send()
-                return c
-
-            lax.fori_loop(0, n, forwarded, 0)
-
-            def parted(t, c, q=q):
-                partial_copy(q, t, dp).wait_send()
-                return c
-
-            lax.fori_loop(0, groups, parted, 0)
+        landed(snd.at[pl.ds(0, n - 1)], d_send)
+        landed(zrx.at[pl.ds(0, n - 1)], z_send)
+        landed(rx.at[pl.ds(0, dpn - 1)], f_send)
+        landed(px.at[pl.ds(0, dpn - 1)], p_send)
+        landed(zdp.at[pl.ds(0, dpn - 1)], y_send)
+        landed(zdp.at[pl.ds(0, dpn - 1)], y_recv)
         loss = zdp[dp]
         for q in range(1, dpn):
-            loss_dp(q, peer_of(q)).wait_recv()
             loss = loss + zdp[peer_of(q)]
-        z_ref[...] = loss[0:1, 0:1] / F32(rows * n * dpn)
+        zout[...] = loss[0:1, 0:1] / F32(rows * n * dpn)
+        z_copy.start()
 
     steps = {
         "send": send_group, "got": arrive, "own": own_part, "peer": peer_part,
@@ -459,12 +437,9 @@
             else:
                 steps[op](at[0] + inner * (at[1] - at[0]), *more)
 
-    def returned(j, c):
-        give_back((me + j) % n, me).wait_send()
-        return c
-
-    with jax.named_scope("finalwait"):
-        lax.fori_loop(1, n, returned, 0)
+    z_copy.wait()
+
+    landed(fin.at[pl.ds(0, n - 1)], r_send)
 
 
 def on_device(n, dpn, tokens, router_weight, route_ids, gate_weight, up_weight, down_weight):
@@ -491,29 +466,32 @@
             pltpu.VMEM((rows, width), BF16),
             jax.ShapeDtypeStruct((1, 1), F32),
         ),
-        in_specs=[vmem, vmem, vmem, hbm, hbm, hbm],
-        out_specs=(vmem, vmem),
+        in_specs=[hbm] * 6,
+        out_specs=(vmem, hbm),
         scratch_shapes=[
+            pltpu.VMEM((rows, width), BF16),
+            pltpu.VMEM((experts, width), BF16),
+            pltpu.VMEM((topk, rows), jnp.int32),
             pltpu.VMEM((n, TILE, block), BF16),
             pltpu.VMEM((dpn, n, TILE, block), BF16),
             pltpu.VMEM((dpn, n, TILE, block), BF16),
             pltpu.VMEM((n, TILE, block), BF16),
             pltpu.VMEM((n, TILE, block), BF16),
             pltpu.VMEM((groups, in_rows, width), F32),
-            pltpu.VMEM((hidden, width), BF16),
-            pltpu.VMEM((hidden, width), BF16),
-            pltpu.VMEM((hidden, width), BF16),
+            pltpu.VMEM((3, hidden, width), BF16),
             pltpu.VMEM((8, 128), F32),
             pltpu.VMEM((n, 8, 128), F32),
             pltpu.VMEM((8, 128), F32),
             pltpu.VMEM((dpn, 8, 128), F32),
-            dma((n,)), dma((n,)), dma((dpn, n)), dma((dpn, n)),
-            dma((dpn, groups)), dma((dpn, groups)), dma((n,)), dma((n,)),
-            dma((n,)), dma((n,)), dma((dpn,)), dma((dpn,)), dma((3,)),
+            dma, dma((n,)), dma, dma((dpn - 1, groups)),
+            dma, dma((dpn - 1, groups)), dma, dma((groups,)),
+            dma, dma, dma, dma, dma, dma((3,)),
             pltpu.VMEM((mains + (TILE // slot if rest else 0), rows, n * TILE), BF16),
             pltpu.VMEM((mains + (TILE // slot if rest else 0), rows, n * TILE), BF16),
             pltpu.VMEM((mains + (TILE // slot if rest else 0), groups, rows, 2 * size * TILE), BF16),
             pltpu.VMEM((rows, width), F32),
+            pltpu.VMEM((1, 1), F32),
+            dma,
         ],
         compiler_params=pltpu.CompilerParams(
             collective_id=0, has_side_effects=True, vmem_limit_bytes=60 * 1024 * 1024

time: 81.5 us -> 77.4 us (0.950)
  the two profiles are of different devices: /device:TPU:9 before, /device:TPU:0 now
where the time goes in v2:
time: 77.4 us; the launch traced here: 76.4 us
  Pallas kernels  73.2 us (95%)
  between operations  2.33 us (3%)
  local copies, waits for them, and re-layouts  0.8 us (1%)
    pallas_call x1, Pallas kernels, on_device(): pl.pallas_call(functools.partial(kernel, n, dpn, cap, groups), out_shape=...  73.2 us

profile of v2, /device:TPU:0, one launch (start us, length us, event | category | flops | bytes accessed | tf_op | source)
XLA Modules:
  0.0 76.4 jit_solution(862085053247581503)
XLA Ops:
  0.6 73.2 %shard_map.77 = (bf16[128,2048]{1,0:T(8,128)(2,1)S(1)}, f32[1,1]{1,0:T(1,128)}) custom-call(bf16[128,2048]{1,0:T(8,128)(2,1)} %tok_hbm.1, bf16[16,2048]{1,0:T(8,128)(2,1)} %bitcast.3, s32[2,128]{1,0:T(2,128)} %bitcast.4, bf16[1,384,2048]{2,1,0:T(8,128)(2,1)} %gate_hbm.1, bf16[1,384,2048]{2,1,0:T(8,128)(2,1)} %up_hbm.1, bf16[1,384,2048]{2,1,0:T(8,128)(2,1)} %down_hbm.1), custom_call_target="tpu_custom_call" | custom-call | tf_op jit(solution)/shard_map/pallas_call | solution.py:463
  73.9 0.8 %copy.10 = bf16[128,2048]{1,0:T(8,128)(2,1)} copy(bf16[128,2048]{1,0:T(8,128)(2,1)S(1)} %get-tuple-element.6) | data formatting | bytes 1048576

commit v3 on v2

--- a/solution.py
+++ b/solution.py
@@ -18,14 +18,17 @@
     ("got", (1, 2), 0), ("got", (1, 2), 1), ("route", 0), ("got", (1, 2), 2), ("got", (1, 2), 3),
     ("own", (1, 2)), ("peer", 0),
     ("got", (2, 1), 0), ("got", (2, 1), 1),
-    ("weigh", 0), ("peer", (1, 2)), ("part", (NO, 2)),
-    ("got", (2, NO), 2), ("got", (2, NO), 3), ("own", (2, NO)),
+    ("weigh", 0), ("peer", (1, 2)), ("part", (NO, 2), 0), ("part", (NO, 2), 1),
+    ("got", (2, 1), 2), ("got", (2, 1), 3), ("own", (2, 1)),
     ("got", 3, 0), ("got", 3, 1), ("got", 3, 2), ("got", 3, 3),
-    ("peer", (2, NO)), ("part", (2, NO)), ("got", (NO, 1), 2), ("got", (NO, 1), 3),
-    ("own", 3), ("end", (NO, 2)), ("own", (NO, 1)), ("peer", 3), ("part", 3), ("part", (1, NO)),
-    ("peer", (NO, 1)), ("part", (NO, 1)), ("part", 0), ("end", (2, NO)),
-    ("end", 3), ("loss", 0), ("done", (2,)), ("end", 1), ("end", 0),
-    ("drain", 0), ("done", (3,)), ("done", (1,)), ("done", (0,)),
+    ("peer", (2, NO)), ("part", (2, NO), 0), ("part", (2, NO), 1),
+    ("own", 3), ("end", (NO, 2), 0), ("end", (NO, 2), 1),
+    ("peer", (NO, 1)), ("part", (NO, 1), 0), ("part", (NO, 1), 1),
+    ("peer", 3), ("part", 3, 0), ("part", 3, 1), ("part", (1, NO), 0), ("part", (1, NO), 1),
+    ("part", 0, 0), ("part", 0, 1),
+    ("end", (2, 1), 0), ("end", (2, 1), 1), ("end", 3, 0), ("end", 3, 1), ("loss", 0),
+    ("end", (1, NO), 0), ("end", (1, NO), 1), ("end", 0, 0), ("done", (2,)), ("end", 0, 1),
+    ("drain", 0), ("done", (1,)), ("done", (3,)), ("done", (0,)),
 )
 PLAN_ONE = tuple(
     (op, (0,) if op == "done" else 0) + ((True,) if op == "send" else ())
@@ -184,13 +187,25 @@
             for q in range(1, dpn):
                 forward(q, me, dp).start()
 
+    def order_of(blocks):
+        full = blocks * TILE
+        at_row, at_col = iota((full, full), 0), iota((full, full), 1)
+        per_cut = blocks * slot
+        want = ((at_row % per_cut) // slot) * TILE + (at_row // per_cut) * slot + at_row % slot
+        return (at_col == want).astype(F32).astype(BF16)
+
+    def part_of(k, half):
+        if half is None:
+            return zone_of(k) * size, size, 0
+        near = lane // (size // 2)
+        side = near if half else (near + 1) % 2
+        return zone_of(k) * size + side * (size // 2), size // 2, side
+
     count = size * TILE
-    at_row, at_col = iota((count, count), 0), iota((count, count), 1)
-    per_cut = size * slot
-    want = ((at_row % per_cut) // slot) * TILE + (at_row // per_cut) * slot + at_row % slot
-    order = (at_col == want).astype(F32).astype(BF16)
 
     def natural(block):
+        blocks = block.shape[0]
+        count, per_cut, order = blocks * TILE, blocks * slot, order_of(blocks)
         pieces = [
             block[:, :, m * width : (m + 1) * width].reshape(count, width)
             for m in range(mains)
@@ -205,19 +220,20 @@
             )
         return pieces
 
-    def blocks_of(rows_out, store):
+    def blocks_of(rows_out, blocks, store):
+        count, order = blocks * TILE, order_of(blocks)
         for m in range(mains):
             store(
                 m * width, width,
-                rows_out[m * count : (m + 1) * count].reshape(size, TILE, width),
+                rows_out[m * count : (m + 1) * count].reshape(blocks, TILE, width),
             )
         if rest:
-            tail = rows_out[mains * count :]
+            extra = rows_out[mains * count :]
             stacked = jnp.concatenate(
-                [tail[:, c * part : (c + 1) * part] for c in range(cuts)], axis=0
+                [extra[:, c * part : (c + 1) * part] for c in range(cuts)], axis=0
             )
             mixed = dot(order, stacked, ((0,), (0,))).astype(BF16)
-            store(base, part, mixed.reshape(size, TILE, part))
+            store(base, part, mixed.reshape(blocks, TILE, part))
 
     def expert(block):
         x = jnp.concatenate(natural(block), axis=0)
@@ -227,13 +243,11 @@
         return dot(hidden, ffn_ref[2])
 
     def partial_copy(j, t, half):
-        if half is None:
-            mine = pl.ds(zone_of(t) * size, size)
-        else:
-            mine = pl.ds(zone_of(t) * size + half * (size // 2), size // 2)
+        first, blocks, _ = part_of(t, half)
+        mine = pl.ds(first, blocks)
         return pltpu.make_async_remote_copy(
             src_ref=rx.at[peer_of(j), mine], dst_ref=px.at[dp, mine],
-            send_sem=p_send, recv_sem=p_recv.at[dpn - 1 - j, zone_of(t)],
+            send_sem=p_send, recv_sem=p_recv.at[dpn - 1 - j, zone_of(t), half or 0],
             device_id={"dp": peer_of(j)}, device_id_type=MESH,
         )
 
@@ -328,7 +342,7 @@
             def store(start, wide, value):
                 rx[whose, pl.ds(first, size), :, start : start + wide] = value
 
-            blocks_of(out, store)
+            blocks_of(out, size, store)
             return c
 
         lax.fori_loop(1, dpn, one, 0)
@@ -337,25 +351,34 @@
         for q in range(1, dpn):
             partial_copy(q, k, half).start()
 
-    def finish(k):
-        first = zone_of(k) * size
-        total = own[k]
+    def finish(k, half=None):
+        first, blocks, side = part_of(k, half)
+        if half is None:
+            total = own[k]
+        else:
+            total = []
+            for at, tall in [(m * count, blocks * TILE) for m in range(mains)] + (
+                [(mains * count, blocks * slot)] if rest else []
+            ):
+                total.append(own[k, pl.ds(pl.multiple_of(at + side * tall, 8), tall), :])
+            total = jnp.concatenate(total, axis=0)
         for q in range(1, dpn):
-            landed(px.at[peer_of(q), pl.ds(first, size)], p_recv.at[q - 1, zone_of(k)])
-            block = px[peer_of(q), pl.ds(first, size)]
-            total = total + jnp.concatenate(natural(block), axis=0).astype(F32)
+            block = px.at[peer_of(q), pl.ds(first, blocks)]
+            landed(block, p_recv.at[q - 1, zone_of(k), half or 0])
+            total = total + jnp.concatenate(natural(block[...]), axis=0).astype(F32)
 
         def store(start, wide, value):
-            fin[pl.ds(first, size), :, start : start + wide] = value
-
-        blocks_of(total.astype(BF16), store)
+            fin[pl.ds(first, blocks), :, start : start + wide] = value
+
+        blocks_of(total.astype(BF16), blocks, store)
+        mixed = home(k) and half != 0
 
         def back(j, c):
-            give_back(first + (lane + j) % size, me).start()
+            give_back(first + (lane % blocks + j) % blocks, me).start()
             return c
 
-        lax.fori_loop(1 if home(k) else 0, size, back, 0)
-        if home(k):
+        lax.fori_loop(1 if mixed else 0, blocks, back, 0)
+        if mixed:
             ret[me] = fin[me]
 
     def cut(i, k):
@@ -484,7 +507,7 @@
             pltpu.VMEM((8, 128), F32),
             pltpu.VMEM((dpn, 8, 128), F32),
             dma, dma((n,)), dma, dma((dpn - 1, groups)),
-            dma, dma((dpn - 1, groups)), dma, dma((groups,)),
+            dma, dma((dpn - 1, groups, 2)), dma, dma((groups,)),
             dma, dma, dma, dma, dma, dma((3,)),
             pltpu.VMEM((mains + (TILE // slot if rest else 0), rows, n * TILE), BF16),
             pltpu.VMEM((mains + (TILE // slot if rest else 0), rows, n * TILE), BF16),

time: 77.4 us -> 73.9 us (0.955); the launches traced: 76.4 us -> 73.7 us
  Pallas kernels: 73.2 us -> 70.6 us
    pallas_call x1, Pallas kernels: 73.2 us -> 70.6 us  [on_device(): pl.pallas_call(functools.partial(kernel, n, dpn, cap, groups), out_shape=...]
where the time goes in v3:
time: 73.9 us; the launch traced here: 73.7 us
  Pallas kernels  70.6 us (96%)
  between operations  2.33 us (3%)
  local copies, waits for them, and re-layouts  0.8 us (1%)
    pallas_call x1, Pallas kernels, on_device(): pl.pallas_call(functools.partial(kernel, n, dpn, cap, groups), out_shape=...  70.6 us

profile of v3, /device:TPU:0, one launch (start us, length us, event | category | flops | bytes accessed | tf_op | source)
XLA Modules:
  0.0 73.7 jit_solution(7683049318963885349)
XLA Ops:
  0.6 70.6 %shard_map.77 = (bf16[128,2048]{1,0:T(8,128)(2,1)S(1)}, f32[1,1]{1,0:T(1,128)}) custom-call(bf16[128,2048]{1,0:T(8,128)(2,1)} %tok_hbm.1, bf16[16,2048]{1,0:T(8,128)(2,1)} %bitcast.3, s32[2,128]{1,0:T(2,128)} %bitcast.4, bf16[1,384,2048]{2,1,0:T(8,128)(2,1)} %gate_hbm.1, bf16[1,384,2048]{2,1,0:T(8,128)(2,1)} %up_hbm.1, bf16[1,384,2048]{2,1,0:T(8,128)(2,1)} %down_hbm.1), custom_call_target="tpu_custom_call" | custom-call | tf_op jit(solution)/shard_map/pallas_call | solution.py:486
  71.2 0.8 %copy.10 = bf16[128,2048]{1,0:T(8,128)(2,1)} copy(bf16[128,2048]{1,0:T(8,128)(2,1)S(1)} %get-tuple-element.6) | data formatting | bytes 1048576

commit v4 on v3

--- a/solution.py
+++ b/solution.py
@@ -20,14 +20,14 @@
     ("got", (2, 1), 0), ("got", (2, 1), 1),
     ("weigh", 0), ("peer", (1, 2)), ("part", (NO, 2), 0), ("part", (NO, 2), 1),
     ("got", (2, 1), 2), ("got", (2, 1), 3), ("own", (2, 1)),
-    ("got", 3, 0), ("got", 3, 1), ("got", 3, 2), ("got", 3, 3),
+    ("got", 3, 0), ("got", 3, 1), ("end", (NO, 2), 0), ("got", 3, 2), ("end", (NO, 2), 1), ("got", 3, 3),
     ("peer", (2, NO)), ("part", (2, NO), 0), ("part", (2, NO), 1),
-    ("own", 3), ("end", (NO, 2), 0), ("end", (NO, 2), 1),
+    ("own", 3),
     ("peer", (NO, 1)), ("part", (NO, 1), 0), ("part", (NO, 1), 1),
-    ("peer", 3), ("part", 3, 0), ("part", 3, 1), ("part", (1, NO), 0), ("part", (1, NO), 1),
-    ("part", 0, 0), ("part", 0, 1),
+    ("peer", 3), ("part", 3, 0), ("part", 3, 1), ("part", (1, NO), 0), ("part", 0, 0), ("part", (1, NO), 1),
+    ("part", 0, 1),
     ("end", (2, 1), 0), ("end", (2, 1), 1), ("end", 3, 0), ("end", 3, 1), ("loss", 0),
-    ("end", (1, NO), 0), ("end", (1, NO), 1), ("end", 0, 0), ("done", (2,)), ("end", 0, 1),
+    ("end", (1, NO), 0), ("end", 0, 0), ("end", (1, NO), 1), ("done", (2,)), ("end", 0, 1),
     ("drain", 0), ("done", (1,)), ("done", (3,)), ("done", (0,)),
 )
 PLAN_ONE = tuple(
@@ -95,8 +95,6 @@
     ]
     for load in inputs:
         load.start()
-    for i, src in enumerate((gate_hbm, up_hbm, down_hbm)):
-        pltpu.make_async_copy(src.at[0], ffn_ref.at[i], w_sem).start()
 
     z_copy = pltpu.make_async_copy(zout, z_ref, o_sem)
     barrier = pltpu.get_barrier_semaphore()
@@ -134,7 +132,8 @@
         return out
 
     inputs[1].wait()
-    inputs[2].wait()
+    for i, src in enumerate((gate_hbm, up_hbm, down_hbm)):
+        pltpu.make_async_copy(src.at[0], ffn_ref.at[i], w_sem).start()
     goal_t = [targets(ids_ref[k : k + 1, :], pos_t[k]) for k in range(topk)]
     row_at = iota((size * TILE, rows), 0)
 
@@ -273,6 +272,7 @@
         )
 
     def route():
+        inputs[2].wait()
         logits = dot(tok_ref[...], router_ref[...], ((1,), (1,)))
         top = jnp.max(logits, axis=1, keepdims=True)
         log_total = top + jnp.log(jnp.sum(jnp.exp(logits - top), axis=1, keepdims=True))

time: 73.9 us -> 72.3 us (0.978)
  Pallas kernels: 70.6 us -> 69 us
    pallas_call x1, Pallas kernels: 70.6 us -> 69 us  [on_device(): pl.pallas_call(functools.partial(kernel, n, dpn, cap, groups), out_shape=...]
where the time goes in v4:
time: 72.3 us; the launch traced here: 72.1 us
  Pallas kernels  69 us (95%)
  between operations  2.33 us (3%)
  local copies, waits for them, and re-layouts  0.8 us (1%)
    pallas_call x1, Pallas kernels, on_device(): pl.pallas_call(functools.partial(kernel, n, dpn, cap, groups), out_shape=...  69 us

profile of v4, /device:TPU:0, one launch (start us, length us, event | category | flops | bytes accessed | tf_op | source)
XLA Modules:
  0.0 72.1 jit_solution(15570630502469157648)
XLA Ops:
  0.6 69.0 %shard_map.77 = (bf16[128,2048]{1,0:T(8,128)(2,1)S(1)}, f32[1,1]{1,0:T(1,128)}) custom-call(bf16[128,2048]{1,0:T(8,128)(2,1)} %tok_hbm.1, bf16[16,2048]{1,0:T(8,128)(2,1)} %bitcast.3, s32[2,128]{1,0:T(2,128)} %bitcast.4, bf16[1,384,2048]{2,1,0:T(8,128)(2,1)} %gate_hbm.1, bf16[1,384,2048]{2,1,0:T(8,128)(2,1)} %up_hbm.1, bf16[1,384,2048]{2,1,0:T(8,128)(2,1)} %down_hbm.1), custom_call_target="tpu_custom_call" | custom-call | tf_op jit(solution)/shard_map/pallas_call | solution.py:486
  69.6 0.8 %copy.10 = bf16[128,2048]{1,0:T(8,128)(2,1)} copy(bf16[128,2048]{1,0:T(8,128)(2,1)S(1)} %get-tuple-element.6) | data formatting | bytes 1048576

commit v5 on v4

--- a/solution.py
+++ b/solution.py
@@ -13,26 +13,26 @@
 TILE = 16
 NO = None
 PLAN = (
-    ("send", (2, 1), True), ("send", 0), ("send", (1, 2)), ("send", 3),
-    ("load", 0), ("got", 0), ("own", 0),
-    ("got", (1, 2), 0), ("got", (1, 2), 1), ("route", 0), ("got", (1, 2), 2), ("got", (1, 2), 3),
-    ("own", (1, 2)), ("peer", 0),
-    ("got", (2, 1), 0), ("got", (2, 1), 1),
-    ("weigh", 0), ("peer", (1, 2)), ("part", (NO, 2), 0), ("part", (NO, 2), 1),
-    ("got", (2, 1), 2), ("got", (2, 1), 3), ("own", (2, 1)),
-    ("got", 3, 0), ("got", 3, 1), ("end", (NO, 2), 0), ("got", 3, 2), ("end", (NO, 2), 1), ("got", 3, 3),
-    ("peer", (2, NO)), ("part", (2, NO), 0), ("part", (2, NO), 1),
-    ("own", 3),
-    ("peer", (NO, 1)), ("part", (NO, 1), 0), ("part", (NO, 1), 1),
-    ("peer", 3), ("part", 3, 0), ("part", 3, 1), ("part", (1, NO), 0), ("part", 0, 0), ("part", (1, NO), 1),
-    ("part", 0, 1),
-    ("end", (2, 1), 0), ("end", (2, 1), 1), ("end", 3, 0), ("end", 3, 1), ("loss", 0),
-    ("end", (1, NO), 0), ("end", 0, 0), ("end", (1, NO), 1), ("done", (2,)), ("end", 0, 1),
-    ("drain", 0), ("done", (1,)), ("done", (3,)), ("done", (0,)),
+    ("share", 0, True), ("send", (2, 1)), ("share", 1), ("send", 0), ("send", (1, 2)), ("send", 3),
+    ("share", (2, NO)), ("share", (3, NO)),
+    ("load", 0), ("pass", (NO, 2), 0), ("pass", (NO, 2), 1), ("pass", (NO, 2), 2), ("pass", (NO, 2), 3),
+    ("share", (NO, 2)), ("share", (NO, 3)), ("got", 0), ("own", 0), ("route", 0),
+    ("got", (1, NO)), ("own", (1, 2)), ("weigh", 0),
+    ("pass", (2, NO), 0), ("pass", (2, NO), 1),
+    ("peer", (NO, 2)), ("part", (NO, 2), 0), ("part", (NO, 2), 1), ("relay", 0),
+    ("pass", (2, NO), 2), ("pass", (2, NO), 3), ("got", (NO, 1)), ("own", (2, 1)),
+    ("pass", 3, 0), ("pass", 3, 1), ("end", (NO, 2), 0), ("pass", 3, 2), ("end", (NO, 2), 1), ("pass", 3, 3),
+    ("own", (NO, 3)), ("peer", (2, 1)), ("part", (2, 1), 0), ("part", (2, 1), 1), ("own", (3, NO)),
+    ("peer", 3), ("part", 3, 0), ("part", 3, 1), ("end", (2, NO), 0),
+    ("peer", (1, 0)), ("part", (1, 0), 0),
+    ("peer", (0, NO)), ("part", (0, NO), 0), ("part", (1, NO), 1), ("part", 0, 1),
+    ("end", (2, 1), (1, 0)), ("end", (3, 1), (0, 1)), ("loss", 0), ("end", 3, (1, 0)),
+    ("end", (1, 3), (0, 1)), ("end", 0, 0), ("end", (1, NO), 1), ("done", 2, "first"), ("end", 0, 1),
+    ("drain", 0), ("done", (3, 1)), ("done", 0), ("done", (1, 3), "last"),
 )
-PLAN_ONE = tuple(
-    (op, (0,) if op == "done" else 0) + ((True,) if op == "send" else ())
-    for op in ("send", "load", "got", "route", "weigh", "own", "peer", "part", "end", "loss", "drain", "done")
+ORDER_ONE = ("send", "load", "relay", "got", "route", "weigh", "own", "peer", "part", "end", "loss", "drain", "done")
+PLAN_ONE = (("share", 0, True), ("share", 1), ("share", 2), ("share", 3)) + tuple(
+    (op, 0, "only") if op == "done" else (op, 0) for op in ORDER_ONE
 )
 
 
@@ -52,6 +52,7 @@
     d_send, d_recv, f_send, f_recv, p_send, p_recv, r_send, r_recv,
     z_send, z_recv, y_send, y_recv, w_sem, i_sem,
     hi_ref, lo_ref, w_ref, acc_ref, zout, o_sem,
+    peer_tok, peer_ids, out_ref, s_send, s_recv, t_send, t_recv, e_send,
 ):
     rows, width = tok_hbm.shape
     topk = ids_hbm.shape[0]
@@ -71,7 +72,8 @@
 
     plan = PLAN if groups == 4 else PLAN_ONE
     inner = ((zone + 1) // 2) % 2 if groups == 4 else 0
-    tail = [step[1] for step in plan if step[0] == "done"]
+
+    near = 2 if groups == 4 else 1
 
     def home(k):
         return isinstance(k, int) and k == 0
@@ -112,14 +114,19 @@
         )
 
     inputs[0].wait()
-    hot_t = [(ids_ref[k : k + 1, :] == iota((n, rows), 0)) for k in range(topk)]
-    all_t = sum(h.astype(F32) for h in hot_t).astype(BF16)
     upper = (iota((rows, rows), 0) < iota((rows, rows), 1)).astype(F32).astype(BF16)
-    before_t = dot(all_t, upper)
-    pos_t = [
-        jnp.sum(jnp.where(h, before_t, 0.0), axis=0, keepdims=True).astype(jnp.int32)
-        for h in hot_t
-    ]
+
+    def hot_of(ids):
+        return [(ids[k : k + 1, :] == iota((n, rows), 0)) for k in range(topk)]
+
+    def goals(ids):
+        hot = hot_of(ids)
+        before = dot(sum(h.astype(F32) for h in hot).astype(BF16), upper)
+        pos = [
+            jnp.sum(jnp.where(h, before, 0.0), axis=0, keepdims=True).astype(jnp.int32)
+            for h in hot
+        ]
+        return [targets(ids[k : k + 1, :], pos[k]) for k in range(topk)]
 
     def targets(ids, pos):
         out = []
@@ -131,10 +138,11 @@
             out.append(jnp.where(inside, ids * TILE + c * slot + pos - mains * TILE, -1))
         return out
 
+    hot_t = hot_of(ids_ref[...])
+    goal_t = goals(ids_ref[...])
     inputs[1].wait()
     for i, src in enumerate((gate_hbm, up_hbm, down_hbm)):
         pltpu.make_async_copy(src.at[0], ffn_ref.at[i], w_sem).start()
-    goal_t = [targets(ids_ref[k : k + 1, :], pos_t[k]) for k in range(topk)]
     row_at = iota((size * TILE, rows), 0)
 
     def dispatch(to, at):
@@ -151,29 +159,31 @@
             device_id={"dp": peer_of(j)}, device_id_type=MESH,
         )
 
-    def send_group(k, entry=False):
-        first = zone_of(k) * size
-        mine = pl.ds(first, size)
-
+    def gather(tokens, goal, first, store):
         def pick(i):
             at = row_at + first * TILE
-            hit = at == goal_t[0][i]
+            hit = at == goal[0][i]
             for c in range(1, topk):
-                hit = hit | (at == goal_t[c][i])
+                hit = hit | (at == goal[c][i])
             return hit.astype(F32).astype(BF16)
 
         for m in range(mains):
-            snd[mine, :, m * width : (m + 1) * width] = (
-                dot(pick(m), tok_ref[...]).astype(BF16).reshape(size, TILE, width)
-            )
+            chosen = dot(pick(m), tokens[...]).astype(BF16)
+            store(m * width, width, chosen.reshape(size, TILE, width))
         if rest:
             extra = sum(
-                dot(pick(mains + c), tok_ref[:, c * part : (c + 1) * part])
+                dot(pick(mains + c), tokens[:, c * part : (c + 1) * part])
                 for c in range(cuts)
             )
-            snd[mine, :, base:] = extra.astype(BF16).reshape(size, TILE, part)
-        if entry:
-            pl.semaphore_wait(barrier, n - 1 + dpn - 1)
+            store(base, part, extra.astype(BF16).reshape(size, TILE, part))
+
+    def send_group(k):
+        first = zone_of(k) * size
+
+        def store(start, wide, value):
+            snd[pl.ds(first, size), :, start : start + wide] = value
+
+        gather(tok_ref, goal_t, first, store)
 
         def one(j, c):
             to = first + (lane + j) % size
@@ -183,8 +193,52 @@
         lax.fori_loop(1 if home(k) else 0, size, one, 0)
         if home(k):
             rx[dp, me] = snd[me]
-            for q in range(1, dpn):
-                forward(q, me, dp).start()
+
+    def share(c, entry=False):
+        if entry:
+            pl.semaphore_wait(barrier, n - 1 + dpn - 1)
+        mine = pl.ds(c * (rows // 4), rows // 4)
+        for q in range(1, dpn):
+            pltpu.make_async_remote_copy(
+                src_ref=tok_ref.at[mine], dst_ref=peer_tok.at[dpn - 1 - q, mine],
+                send_sem=s_send, recv_sem=s_recv.at[dpn - 1 - q],
+                device_id={"dp": peer_of(q)}, device_id_type=MESH,
+            ).start()
+            if entry:
+                pltpu.make_async_remote_copy(
+                    src_ref=ids_ref, dst_ref=peer_ids.at[dpn - 1 - q],
+                    send_sem=t_send, recv_sem=t_recv.at[dpn - 1 - q],
+                    device_id={"dp": peer_of(q)}, device_id_type=MESH,
+                ).start()
+
+    def relay(unused):
+        def one_peer(q, c):
+            whose = peer_of(q)
+            landed(peer_ids.at[q - 1], t_recv.at[q - 1])
+            goal = goals(peer_ids[q - 1])
+            landed(peer_tok.at[q - 1], s_recv.at[q - 1])
+            for k in range(near):
+                first = zone_of(k) * size
+
+                def store(start, wide, value, k=k):
+                    out_ref[q - 1, k * size : (k + 1) * size, :, start : start + wide] = value
+
+                gather(peer_tok.at[q - 1], goal, first, store)
+
+                def one(j, c2, k=k, first=first):
+                    to = (lane + j) % size
+                    pltpu.make_async_remote_copy(
+                        src_ref=out_ref.at[q - 1, k * size + to], dst_ref=rx.at[whose, me],
+                        send_sem=e_send, recv_sem=f_recv.at[q - 1, zone],
+                        device_id={"expert": first + to}, device_id_type=MESH,
+                    ).start()
+                    return c2
+
+                lax.fori_loop(1 if k == 0 else 0, size, one, 0)
+            rx[whose, me] = out_ref[q - 1, lane]
+            return c
+
+        lax.fori_loop(1, dpn, one_peer, 0)
 
     def order_of(blocks):
         full = blocks * TILE
@@ -311,13 +365,13 @@
             hi_ref[i] = hi
             lo_ref[i] = (w - hi.astype(F32)).astype(BF16)
 
-    def arrive(k, part=None):
+    def arrive(k, part=None, onward=False):
         first = zone_of(k) * size
 
         def one(j, c):
             at = first + (lane + size - j) % size
             dispatch(at, at).wait_recv()
-            for q in range(1, dpn):
+            for q in range(1, dpn if onward else 1):
                 forward(q, at, dp).start()
             return c
 
@@ -336,7 +390,8 @@
         def one(q, c):
             whose = peer_of(q)
 
-            landed(rx.at[whose, pl.ds(first, size)], f_recv.at[q - 1, zone_of(k)])
+            come = pl.ds(first, size - 1 if home(k) else size)
+            landed(rx.at[whose, come], f_recv.at[q - 1, zone_of(k)])
             out = expert(rx[whose, pl.ds(first, size)]).astype(BF16)
 
             def store(start, wide, value):
@@ -394,26 +449,24 @@
             for k in range(groups):
                 w_ref[i, k] = cut(i, k)
 
-    def take(ks):
-        for k in ks:
-            here = pl.ds(zone_of(k) * size, size - 1 if home(k) else size)
-            landed(ret.at[here], r_recv.at[zone_of(k)])
+    def take(k, place=""):
+        here = pl.ds(zone_of(k) * size, size - 1 if home(k) else size)
+        landed(ret.at[here], r_recv.at[zone_of(k)])
 
         def twice(x):
             return jnp.concatenate([x, x], axis=0)
 
+        mine = pl.ds(zone_of(k) * size, size)
         for c in range(cuts):
             cols = slice(c * part, (c + 1) * part)
-            acc = 0.0 if ks == tail[0] else acc_ref[:, cols]
-            for k in ks:
-                mine = pl.ds(zone_of(k) * size, size)
-                for m in range(mains):
-                    seen = ret[mine, :, m * width + c * part : m * width + (c + 1) * part]
-                    acc = acc + dot(w_ref[m, k], twice(seen.reshape(count, part)))
-                if rest:
-                    seen = ret[mine, :, base:].reshape(count, part)
-                    acc = acc + dot(w_ref[mains + c, k], twice(seen))
-            if ks == tail[-1]:
+            acc = 0.0 if place in ("first", "only") else acc_ref[:, cols]
+            for m in range(mains):
+                seen = ret[mine, :, m * width + c * part : m * width + (c + 1) * part]
+                acc = acc + dot(w_ref[m, k], twice(seen.reshape(count, part)))
+            if rest:
+                seen = ret[mine, :, base:].reshape(count, part)
+                acc = acc + dot(w_ref[mains + c, k], twice(seen))
+            if place in ("last", "only"):
                 mix_ref[:, cols] = acc.astype(BF16)
             else:
                 acc_ref[:, cols] = acc
@@ -435,7 +488,11 @@
     def drain(k):
         landed(snd.at[pl.ds(0, n - 1)], d_send)
         landed(zrx.at[pl.ds(0, n - 1)], z_send)
-        landed(rx.at[pl.ds(0, dpn - 1)], f_send)
+        if groups > near:
+            landed(rx.at[pl.ds(0, dpn - 1), pl.ds(0, (groups - near) * size)], f_send)
+        landed(peer_tok, s_send)
+        landed(peer_ids, t_send)
+        landed(out_ref.at[pl.ds(0, dpn - 1), pl.ds(0, near * size - 1)], e_send)
         landed(px.at[pl.ds(0, dpn - 1)], p_send)
         landed(zdp.at[pl.ds(0, dpn - 1)], y_send)
         landed(zdp.at[pl.ds(0, dpn - 1)], y_recv)
@@ -446,17 +503,22 @@
         z_copy.start()
 
     steps = {
-        "send": send_group, "got": arrive, "own": own_part, "peer": peer_part,
+        "send": send_group, "got": arrive, "share": share, "relay": relay,
+        "pass": functools.partial(arrive, onward=True),
+        "own": own_part, "peer": peer_part,
         "part": send_part, "end": finish, "done": take, "load": loads_in,
         "route": lambda k: route(), "loss": lambda k: gather_loss(), "weigh": weigh, "drain": drain,
     }
     for op, at, *more in plan:
         with jax.named_scope(f"{op}_{at}_{more}"):
-            if op == "done" or not isinstance(at, tuple):
+            split = any(isinstance(m, tuple) for m in more)
+            if not (split or isinstance(at, tuple)):
                 steps[op](at, *more)
-            elif None in at:
-                chosen = at[0] if at[1] is None else at[1]
-                pl.when(inner == at.index(chosen))(functools.partial(steps[op], chosen, *more))
+            elif split or None in at or 0 in at:
+                for kind in range(2):
+                    first, *rest_of = [m[kind] if isinstance(m, tuple) else m for m in (at, *more)]
+                    if first is not None:
+                        pl.when(inner == kind)(functools.partial(steps[op], first, *rest_of))
             else:
                 steps[op](at[0] + inner * (at[1] - at[0]), *more)
 
@@ -515,6 +577,10 @@
             pltpu.VMEM((rows, width), F32),
             pltpu.VMEM((1, 1), F32),
             dma,
+            pltpu.VMEM((dpn - 1, rows, width), BF16),
+            pltpu.VMEM((dpn - 1, topk, rows), jnp.int32),
+            pltpu.VMEM((dpn - 1, (2 if groups == 4 else 1) * size, TILE, block), BF16),
+            dma, dma((dpn - 1,)), dma, dma((dpn - 1,)), dma,
         ],
         compiler_params=pltpu.CompilerParams(
             collective_id=0, has_side_effects=True, vmem_limit_bytes=60 * 1024 * 1024

time: 72.3 us -> 70.1 us (0.970)
  Pallas kernels: 69 us -> 66.8 us
    pallas_call x1, Pallas kernels: 69 us -> 66.8 us  [on_device(): pl.pallas_call(functools.partial(kernel, n, dpn, cap, groups), out_shape=...]
where the time goes in v5:
time: 70.1 us; the launch traced here: 69.9 us
  Pallas kernels  66.8 us (95%)
  between operations  2.33 us (3%)
  local copies, waits for them, and re-layouts  0.8 us (1%)
    pallas_call x1, Pallas kernels, on_device(): pl.pallas_call(functools.partial(kernel, n, dpn, cap, groups), out_shape=...  66.8 us

profile of v5, /device:TPU:0, one launch (start us, length us, event | category | flops | bytes accessed | tf_op | source)
XLA Modules:
  0.0 69.9 jit_solution(16364726897064655091)
XLA Ops:
  0.6 66.8 %shard_map.77 = (bf16[128,2048]{1,0:T(8,128)(2,1)S(1)}, f32[1,1]{1,0:T(1,128)}) custom-call(bf16[128,2048]{1,0:T(8,128)(2,1)} %tok_hbm.1, bf16[16,2048]{1,0:T(8,128)(2,1)} %bitcast.3, s32[2,128]{1,0:T(2,128)} %bitcast.4, bf16[1,384,2048]{2,1,0:T(8,128)(2,1)} %gate_hbm.1, bf16[1,384,2048]{2,1,0:T(8,128)(2,1)} %up_hbm.1, bf16[1,384,2048]{2,1,0:T(8,128)(2,1)} %down_hbm.1), custom_call_target="tpu_custom_call" | custom-call | tf_op jit(solution)/shard_map/pallas_call | solution.py:548
  67.4 0.8 %copy.10 = bf16[128,2048]{1,0:T(8,128)(2,1)} copy(bf16[128,2048]{1,0:T(8,128)(2,1)S(1)} %get-tuple-element.6) | data formatting | bytes 1048576

commit v6 on v5

--- a/solution.py
+++ b/solution.py
@@ -13,22 +13,72 @@
 TILE = 16
 NO = None
 PLAN = (
-    ("share", 0, True), ("send", (2, 1)), ("share", 1), ("send", 0), ("send", (1, 2)), ("send", 3),
-    ("share", (2, NO)), ("share", (3, NO)),
-    ("load", 0), ("pass", (NO, 2), 0), ("pass", (NO, 2), 1), ("pass", (NO, 2), 2), ("pass", (NO, 2), 3),
-    ("share", (NO, 2)), ("share", (NO, 3)), ("got", 0), ("own", 0), ("route", 0),
-    ("got", (1, NO)), ("own", (1, 2)), ("weigh", 0),
-    ("pass", (2, NO), 0), ("pass", (2, NO), 1),
-    ("peer", (NO, 2)), ("part", (NO, 2), 0), ("part", (NO, 2), 1), ("relay", 0),
-    ("pass", (2, NO), 2), ("pass", (2, NO), 3), ("got", (NO, 1)), ("own", (2, 1)),
-    ("pass", 3, 0), ("pass", 3, 1), ("end", (NO, 2), 0), ("pass", 3, 2), ("end", (NO, 2), 1), ("pass", 3, 3),
-    ("own", (NO, 3)), ("peer", (2, 1)), ("part", (2, 1), 0), ("part", (2, 1), 1), ("own", (3, NO)),
-    ("peer", 3), ("part", 3, 0), ("part", 3, 1), ("end", (2, NO), 0),
-    ("peer", (1, 0)), ("part", (1, 0), 0),
-    ("peer", (0, NO)), ("part", (0, NO), 0), ("part", (1, NO), 1), ("part", 0, 1),
-    ("end", (2, 1), (1, 0)), ("end", (3, 1), (0, 1)), ("loss", 0), ("end", 3, (1, 0)),
-    ("end", (1, 3), (0, 1)), ("end", 0, 0), ("end", (1, NO), 1), ("done", 2, "first"), ("end", 0, 1),
-    ("drain", 0), ("done", (3, 1)), ("done", 0), ("done", (1, 3), "last"),
+    ('share', 0, True),
+    ('send', (2, 1)),
+    ('share', 1),
+    ('send', 0),
+    ('send', (1, 2)),
+    ('pass', (None, 2), 1),
+    ('send', 3),
+    ('load', (None, 0)),
+    ('pass', (None, 2), 0),
+    ('pass', (None, 2), 2),
+    ('pass', (None, 2), 3),
+    ('share', 2),
+    ('share', 3),
+    ('load', (0, None)),
+    ('got', 0),
+    ('own', 0),
+    ('route', 0),
+    ('got', (1, None)),
+    ('pass', (2, None), 1),
+    ('own', (1, 2)),
+    ('weigh', 0),
+    ('pass', (2, None), 0),
+    ('peer', (None, 2)),
+    ('part', (None, 2), 0),
+    ('part', (None, 2), 1),
+    ('relay', 0),
+    ('pass', (2, None), 2),
+    ('pass', (2, None), 3),
+    ('got', (None, 1)),
+    ('own', (2, 1)),
+    ('pass', 3, 0),
+    ('pass', 3, 1),
+    ('end', (None, 2), 0),
+    ('pass', 3, 2),
+    ('end', (None, 2), 1),
+    ('pass', 3, 3),
+    ('peer', (2, None)),
+    ('part', (2, None), 0),
+    ('part', (2, None), 1),
+    ('own', 3),
+    ('peer', (3, 1)),
+    ('part', (3, 1), 0),
+    ('part', (3, 1), 1),
+    ('end', (2, None), 0),
+    ('peer', (1, 3)),
+    ('part', (1, 3), 0),
+    ('part', (None, 3), 1),
+    ('peer', 0),
+    ('part', 0, 0),
+    ('part', (1, None), 1),
+    ('part', 0, 1),
+    ('end', (2, None), 1),
+    ('end', (3, 1), 0),
+    ('loss', (0, None)),
+    ('end', (3, 1), 1),
+    ('loss', (None, 0)),
+    ('end', (1, 3), 0),
+    ('end', (0, None), 0),
+    ('end', (1, 3), 1),
+    ('end', (None, 0), 0),
+    ('done', 2, 'first'),
+    ('end', 0, 1),
+    ('drain', 0),
+    ('done', (3, 1)),
+    ('done', 0),
+    ('done', (1, 3), 'last'),
 )
 ORDER_ONE = ("send", "load", "relay", "got", "route", "weigh", "own", "peer", "part", "end", "loss", "drain", "done")
 PLAN_ONE = (("share", 0, True), ("share", 1), ("share", 2), ("share", 3)) + tuple(

time: 70.1 us -> 69.4 us (0.990)
  Pallas kernels: 66.8 us -> 65.7 us
    pallas_call x1, Pallas kernels: 66.8 us -> 65.7 us  [on_device(): pl.pallas_call(functools.partial(kernel, n, dpn, cap, groups), out_shape=...]
where the time goes in v6:
time: 69.4 us; the launch traced here: 68.9 us
  Pallas kernels  65.7 us (95%)
  between operations  2.33 us (3%)
  local copies, waits for them, and re-layouts  0.8 us (1%)
    pallas_call x1, Pallas kernels, on_device(): pl.pallas_call(functools.partial(kernel, n, dpn, cap, groups), out_shape=...  65.7 us

profile of v6, /device:TPU:0, one launch (start us, length us, event | category | flops | bytes accessed | tf_op | source)
XLA Modules:
  0.0 68.9 jit_solution(8318462722927789025)
XLA Ops:
  0.6 65.7 %shard_map.77 = (bf16[128,2048]{1,0:T(8,128)(2,1)S(1)}, f32[1,1]{1,0:T(1,128)}) custom-call(bf16[128,2048]{1,0:T(8,128)(2,1)} %tok_hbm.1, bf16[16,2048]{1,0:T(8,128)(2,1)} %bitcast.3, s32[2,128]{1,0:T(2,128)} %bitcast.4, bf16[1,384,2048]{2,1,0:T(8,128)(2,1)} %gate_hbm.1, bf16[1,384,2048]{2,1,0:T(8,128)(2,1)} %up_hbm.1, bf16[1,384,2048]{2,1,0:T(8,128)(2,1)} %down_hbm.1), custom_call_target="tpu_custom_call" | custom-call | tf_op jit(solution)/shard_map/pallas_call | solution.py:598
  66.4 0.8 %copy.10 = bf16[128,2048]{1,0:T(8,128)(2,1)} copy(bf16[128,2048]{1,0:T(8,128)(2,1)S(1)} %get-tuple-element.6) | data formatting | bytes 1048576

commit v7 on v6

--- a/solution.py
+++ b/solution.py
@@ -32,15 +32,15 @@
     ('route', 0),
     ('got', (1, None)),
     ('pass', (2, None), 1),
+    ('pass', (2, None), 0),
     ('own', (1, 2)),
     ('weigh', 0),
-    ('pass', (2, None), 0),
+    ('pass', (2, None), 2),
+    ('pass', (2, None), 3),
     ('peer', (None, 2)),
     ('part', (None, 2), 0),
     ('part', (None, 2), 1),
     ('relay', 0),
-    ('pass', (2, None), 2),
-    ('pass', (2, None), 3),
     ('got', (None, 1)),
     ('own', (2, 1)),
     ('pass', 3, 0),

time: 69.4 us -> 69.2 us (level)
  no operation moved by 1% of the time
where the time goes in v7:
time: 69.2 us; the launch traced here: 69 us
  Pallas kernels  65.9 us (95%)
  between operations  2.33 us (3%)
  local copies, waits for them, and re-layouts  0.8 us (1%)
    pallas_call x1, Pallas kernels, on_device(): pl.pallas_call(functools.partial(kernel, n, dpn, cap, groups), out_shape=...  65.9 us

profile of v7, /device:TPU:0, one launch (start us, length us, event | category | flops | bytes accessed | tf_op | source)
XLA Modules:
  0.0 69.0 jit_solution(17557206772984075803)
XLA Ops:
  0.6 65.9 %shard_map.77 = (bf16[128,2048]{1,0:T(8,128)(2,1)S(1)}, f32[1,1]{1,0:T(1,128)}) custom-call(bf16[128,2048]{1,0:T(8,128)(2,1)} %tok_hbm.1, bf16[16,2048]{1,0:T(8,128)(2,1)} %bitcast.3, s32[2,128]{1,0:T(2,128)} %bitcast.4, bf16[1,384,2048]{2,1,0:T(8,128)(2,1)} %gate_hbm.1, bf16[1,384,2048]{2,1,0:T(8,128)(2,1)} %up_hbm.1, bf16[1,384,2048]{2,1,0:T(8,128)(2,1)} %down_hbm.1), custom_call_target="tpu_custom_call" | custom-call | tf_op jit(solution)/shard_map/pallas_call | solution.py:598
  66.5 0.8 %copy.10 = bf16[128,2048]{1,0:T(8,128)(2,1)} copy(bf16[128,2048]{1,0:T(8,128)(2,1)S(1)} %get-tuple-element.6) | data formatting | bytes 1048576

commit v8 on v7

--- a/solution.py
+++ b/solution.py
@@ -22,9 +22,9 @@
     ('send', 3),
     ('load', (None, 0)),
     ('pass', (None, 2), 0),
+    ('share', 2),
     ('pass', (None, 2), 2),
     ('pass', (None, 2), 3),
-    ('share', 2),
     ('share', 3),
     ('load', (0, None)),
     ('got', 0),

time: 69.2 us -> 69.2 us (level)
  no operation moved by 1% of the time
where the time goes in v8:
time: 69.2 us; the launch traced here: 69.1 us
  Pallas kernels  65.9 us (95%)
  between operations  2.33 us (3%)
  local copies, waits for them, and re-layouts  0.8 us (1%)
    pallas_call x1, Pallas kernels, on_device(): pl.pallas_call(functools.partial(kernel, n, dpn, cap, groups), out_shape=...  65.9 us

profile of v8, /device:TPU:0, one launch (start us, length us, event | category | flops | bytes accessed | tf_op | source)
XLA Modules:
  0.0 69.1 jit_solution(13056885244974755960)
XLA Ops:
  0.6 65.9 %shard_map.77 = (bf16[128,2048]{1,0:T(8,128)(2,1)S(1)}, f32[1,1]{1,0:T(1,128)}) custom-call(bf16[128,2048]{1,0:T(8,128)(2,1)} %tok_hbm.1, bf16[16,2048]{1,0:T(8,128)(2,1)} %bitcast.3, s32[2,128]{1,0:T(2,128)} %bitcast.4, bf16[1,384,2048]{2,1,0:T(8,128)(2,1)} %gate_hbm.1, bf16[1,384,2048]{2,1,0:T(8,128)(2,1)} %up_hbm.1, bf16[1,384,2048]{2,1,0:T(8,128)(2,1)} %down_hbm.1), custom_call_target="tpu_custom_call" | custom-call | tf_op jit(solution)/shard_map/pallas_call | solution.py:598
  66.6 0.8 %copy.10 = bf16[128,2048]{1,0:T(8,128)(2,1)} copy(bf16[128,2048]{1,0:T(8,128)(2,1)S(1)} %get-tuple-element.6) | data formatting | bytes 1048576
